TPU v7x, 32 devices: a whole 2x2x4 slice. The times are simulated.
32 devices in a mesh: gx: 4 (over z), gy: 8 (over y, x, core).
Axes of the slice: x: 2, y: 2, z: 4, core: 2. Of those that a mesh axis runs over, the one named last changes fastest.
Arguments:
- features: bfloat16 [40960, 2048], P(('gx', 'gy')), may hold values from -6 to 6
- counts: int32 [32], P(('gx', 'gy')), may hold values from 128 to 1280, as said below
- ref_mean: float32 [2048], replicated, may hold values from -6 to 6
- ref_root: float32 [2048, 2048], P('gx', 'gy'), as said below
Outputs:
- mean: float32 [2048], replicated
- root: float32 [2048, 2048], P('gx', 'gy')
- distance: float32 [], replicated
Inputs may be any that keep to these rules, and one draw needn't show every extreme that they name: Entry b counts the valid rows of shard b, which come first in it; a multiple of 128; some shard is full in every draw. `ref_root`: symmetric and positive definite.
All inputs are finite; a program needn't handle non-finite values.
Results may differ from a plain program's by a relative error of at most 0.0015.
The roundings to bfloat16 on the way count: a program that leaves them out, or rounds other values in their place, can miss the bound.
Values may be sent and summed in bfloat16 or wider, within the bound.
A program may use at most 128 MiB of HBM per device.

v0:
```python
import jax
import jax.numpy as jnp
from jax import lax
from jax.sharding import PartitionSpec as P

ITERS = 4


def product(left, right):
    left_half = left.astype(jnp.bfloat16)
    right_half = right.astype(jnp.bfloat16)
    panel = lax.all_gather(left_half, "gy", axis=1, tiled=True)
    return jnp.dot(
        panel,
        lax.all_gather(right_half, "gx", axis=0, tiled=True),
        preferred_element_type=jnp.float32,
    )


def shards(features, counts, ref_mean, ref_root):
    width = features.shape[1]
    slots = features.shape[0]
    rows_x = lax.axis_size("gx")
    cols_y = lax.axis_size("gy")
    tile_rows = width // rows_x
    tile_cols = width // cols_y
    keep = (jnp.arange(slots, dtype=jnp.int32) < counts[0])[:, None]
    masked = jnp.where(keep, features, jnp.zeros_like(features))
    partial_gram = lax.dot_general(
        masked, features, (((0,), (0,)), ((), ())), preferred_element_type=jnp.float32
    )
    column_total = jnp.sum(masked.astype(jnp.float32), axis=0)
    local_count = counts[0].astype(jnp.float32)
    total, count = lax.psum((column_total, local_count), ("gx", "gy"))
    column_block = lax.psum_scatter(partial_gram, "gy", scatter_dimension=1, tiled=True)
    gram_tile = lax.psum_scatter(column_block, "gx", scatter_dimension=0, tiled=True)
    mean = total / count
    row_start = lax.axis_index("gx") * tile_rows
    col_start = lax.axis_index("gy") * tile_cols
    mean_rows = lax.dynamic_slice_in_dim(mean, row_start, tile_rows, 0)
    mean_cols = lax.dynamic_slice_in_dim(mean, col_start, tile_cols, 0)
    cov_tile = (gram_tile - count * mean_rows[:, None] * mean_cols[None, :]) / (count - 1.0)
    row_ids = jnp.arange(tile_rows, dtype=jnp.int32) + row_start
    col_ids = jnp.arange(tile_cols, dtype=jnp.int32) + col_start
    identity_tile = (row_ids[:, None] == col_ids[None, :]).astype(jnp.float32)
    half = product(cov_tile, ref_root)
    prod = product(ref_root, half)
    square_sum, cov_trace, root_square = lax.psum(
        (jnp.sum(prod * prod), jnp.sum(cov_tile * identity_tile), jnp.sum(ref_root * ref_root)),
        ("gx", "gy"),
    )
    scale = jnp.sqrt(square_sum + 1.0)
    current = prod / scale
    partner = identity_tile
    for step in range(ITERS):
        middle = 1.5 * identity_tile - 0.5 * product(partner, current)
        current, partner = (product(current, middle), product(middle, partner))
    last_trace = lax.psum(jnp.sum(current * identity_tile), ("gx", "gy"))
    root = jnp.sqrt(scale) * current
    distance = (
        jnp.sum((mean - ref_mean) ** 2)
        + cov_trace
        + root_square
        - 2.0 * jnp.sqrt(scale) * last_trace
    ) / 64.0
    return (mean, root, distance)


def solution(mesh):
    return jax.shard_map(
        shards,
        mesh=mesh,
        in_specs=(P(("gx", "gy"), None), P(("gx", "gy")), P(), P("gx", "gy")),
        out_specs=(P(), P("gx", "gy"), P()),
        check_vma=False,
    )
```

profile of v0, /device:TPU:0, one launch (start us, length us, event | category | flops | bytes accessed | tf_op | source)
XLA Modules:
  0.0 1031.6 jit_solution(1172393237996310174)
XLA Ops:
  7.9 18.1 %fusion = f32[2048,2048]{1,0:T(8,128)} fusion(bf16[1280,2048]{1,0:T(8,128)(2,1)} %param.4, pred[1280]{0:T(1024)(128)(4,1)S(1)} %iota_compare_fusion), kind=kOutput, calls=%fused_computation.1 | convolution fusion | flops 10740039680 | bytes 22021376 | tf_op jit(solution)/shard_map/dot_general | solution.py:29
  26.1 118.8 %reduce-scatter.3.cloned.1.call-done = f32[2048,256]{1,0:T(8,128)} async-done(((f32[2048,2048]{1,0:T(8,128)}), f32[2048,256]{1,0:T(8,128)}) %reduce-scatter.3.cloned.1.call-update) | async-done | bytes 2097168 | tf_op jit(solution)/shard_map/reduce_scatter | solution.py:35
  146.4 3.6 convert_reduce_fusion
  150.0 42.2 %all-reduce.1 = (f32[2048]{0:T(1024)S(1)}, f32[]{:T(128)}) all-reduce(f32[2048]{0:T(1024)S(1)} %convert_reduce_fusion, f32[]{:T(128)S(6)} %convert_element_type.69), channel_id=1, replica_groups=mesh['gx'=4,'gy'=8] {'gx','gy'}, use_global_device_ids=true, to_apply=%region_1.2 | all-reduce | flops 2049 | bytes 16392 | tf_op jit(solution)/shard_map/psum | solution.py:34
  197.5 23.1 %all-gather.29.cloned.1.call-done = bf16[2048,256]{1,0:T(8,128)(2,1)} async-done(((bf16[512,256]{1,0:T(8,128)(2,1)}), bf16[2048,256]{1,0:T(8,128)(2,1)}) %all-gather.29.cloned.1.call-update) | async-done | bytes 1048592 | tf_op jit(solution)/shard_map/all_gather | solution.py:15
  220.6 29.8 %all-gather.27.cloned.1.call-done = bf16[512,2048]{1,0:T(8,128)(2,1)} async-done(((bf16[512,256]{1,0:T(8,128)(2,1)}), bf16[512,2048]{1,0:T(8,128)(2,1)}) %all-gather.27.cloned.1.call-update) | async-done | bytes 2097168 | tf_op jit(solution)/shard_map/all_gather | solution.py:12
  254.7 25.6 %all-gather.33.cloned.1.call-done = bf16[512,2048]{1,0:T(8,128)(2,1)} async-done(((bf16[512,256]{1,0:T(8,128)(2,1)}), bf16[512,2048]{1,0:T(8,128)(2,1)}) %all-gather.33.cloned.1.call-update) | async-done | bytes 2097168 | tf_op jit(solution)/shard_map/all_gather | solution.py:12
  280.3 30.0 %all-gather.31.cloned.1.call-done = bf16[2048,256]{1,0:T(8,128)(2,1)} async-done(((bf16[512,256]{1,0:T(8,128)(2,1)}), bf16[2048,256]{1,0:T(8,128)(2,1)}) %all-gather.31.cloned.1.call-update) | async-done | bytes 1048592 | tf_op jit(solution)/shard_map/all_gather | solution.py:15
  313.6 40.4 %psum.44 = f32[]{:T(128)} all-reduce(f32[]{:T(128)} %get-tuple-element.15), channel_id=1, replica_groups=mesh['gx'=4,'gy'=8] {'gx','gy'}, use_global_device_ids=true, to_apply=%region_6.7 | all-reduce | flops 1 | bytes 8 | tf_op jit(solution)/shard_map/psum | solution.py:48
  355.5 27.4 %all-gather.39.cloned.1.call-done = bf16[2048,256]{0,1:T(8,128)(2,1)} async-done(((bf16[512,256]{0,1:T(8,128)(2,1)}), bf16[2048,256]{0,1:T(8,128)(2,1)}) %all-gather.39.cloned.1.call-update) | async-done | bytes 1048592 | tf_op jit(solution)/shard_map/all_gather | solution.py:15
  388.5 25.4 %all-gather.41.cloned.1.call-done = bf16[2048,256]{1,0:T(8,128)(2,1)} async-done(((bf16[512,256]{1,0:T(8,128)(2,1)}), bf16[2048,256]{1,0:T(8,128)(2,1)}) %all-gather.41.cloned.1.call-update) | async-done | bytes 1048592 | tf_op jit(solution)/shard_map/all_gather | solution.py:15
  413.8 29.5 %all-gather.35.cloned.1.call-done = bf16[512,2048]{0,1:T(8,128)(2,1)} async-done(((bf16[512,256]{0,1:T(8,128)(2,1)}), bf16[512,2048]{0,1:T(8,128)(2,1)}) %all-gather.35.cloned.1.call-update) | async-done | bytes 2097168 | tf_op jit(solution)/shard_map/all_gather | solution.py:12
  446.7 26.2 %all-gather.47.cloned.1.call-done = bf16[2048,256]{1,0:T(8,128)(2,1)} async-done(((bf16[512,256]{1,0:T(8,128)(2,1)}), bf16[2048,256]{1,0:T(8,128)(2,1)}) %all-gather.47.cloned.1.call-update) | async-done | bytes 1048592 | tf_op jit(solution)/shard_map/all_gather | solution.py:15
  472.9 29.2 %all-gather.45.cloned.1.call-done = bf16[512,2048]{1,0:T(8,128)(2,1)} async-done(((bf16[512,256]{1,0:T(8,128)(2,1)}), bf16[512,2048]{1,0:T(8,128)(2,1)}) %all-gather.45.cloned.1.call-update) | async-done | bytes 2097168 | tf_op jit(solution)/shard_map/all_gather | solution.py:12
  506.1 26.2 %all-gather.51.cloned.1.call-done = bf16[2048,256]{1,0:T(8,128)(2,1)} async-done(((bf16[512,256]{1,0:T(8,128)(2,1)}), bf16[2048,256]{1,0:T(8,128)(2,1)}) %all-gather.51.cloned.1.call-update) | async-done | bytes 1048592 | tf_op jit(solution)/shard_map/all_gather | solution.py:15
  532.3 29.2 %all-gather.49.cloned.1.call-done = bf16[512,2048]{1,0:T(8,128)(2,1)} async-done(((bf16[512,256]{1,0:T(8,128)(2,1)}), bf16[512,2048]{1,0:T(8,128)(2,1)}) %all-gather.49.cloned.1.call-update) | async-done | bytes 2097168 | tf_op jit(solution)/shard_map/all_gather | solution.py:12
  566.1 25.9 %all-gather.43.cloned.1.call-done = bf16[512,2048]{1,0:T(8,128)(2,1)} async-done(((bf16[512,256]{1,0:T(8,128)(2,1)}), bf16[512,2048]{1,0:T(8,128)(2,1)}) %all-gather.43.cloned.1.call-update) | async-done | bytes 2097168 | tf_op jit(solution)/shard_map/all_gather | solution.py:12
  592.0 29.4 %all-gather.53.cloned.1.call-done = bf16[2048,256]{1,0:T(8,128)(2,1)} async-done(((bf16[512,256]{1,0:T(8,128)(2,1)}), bf16[2048,256]{1,0:T(8,128)(2,1)}) %all-gather.53.cloned.1.call-update) | async-done | bytes 1048592 | tf_op jit(solution)/shard_map/all_gather | solution.py:15
  624.8 25.5 %all-gather.59.cloned.1.call-done = bf16[2048,256]{1,0:T(8,128)(2,1)} async-done(((bf16[512,256]{1,0:T(8,128)(2,1)}), bf16[2048,256]{1,0:T(8,128)(2,1)}) %all-gather.59.cloned.1.call-update) | async-done | bytes 1048592 | tf_op jit(solution)/shard_map/all_gather | solution.py:15
  650.2 29.2 %all-gather.57.cloned.1.call-done = bf16[512,2048]{1,0:T(8,128)(2,1)} async-done(((bf16[512,256]{1,0:T(8,128)(2,1)}), bf16[512,2048]{1,0:T(8,128)(2,1)}) %all-gather.57.cloned.1.call-update) | async-done | bytes 2097168 | tf_op jit(solution)/shard_map/all_gather | solution.py:12
  683.6 26.1 %all-gather.63.cloned.1.call-done = bf16[2048,256]{1,0:T(8,128)(2,1)} async-done(((bf16[512,256]{1,0:T(8,128)(2,1)}), bf16[2048,256]{1,0:T(8,128)(2,1)}) %all-gather.63.cloned.1.call-update) | async-done | bytes 1048592 | tf_op jit(solution)/shard_map/all_gather | solution.py:15
  709.6 29.2 %all-gather.61.cloned.1.call-done = bf16[512,2048]{1,0:T(8,128)(2,1)} async-done(((bf16[512,256]{1,0:T(8,128)(2,1)}), bf16[512,2048]{1,0:T(8,128)(2,1)}) %all-gather.61.cloned.1.call-update) | async-done | bytes 2097168 | tf_op jit(solution)/shard_map/all_gather | solution.py:12
  743.5 25.9 %all-gather.55.cloned.1.call-done = bf16[512,2048]{1,0:T(8,128)(2,1)} async-done(((bf16[512,256]{1,0:T(8,128)(2,1)}), bf16[512,2048]{1,0:T(8,128)(2,1)}) %all-gather.55.cloned.1.call-update) | async-done | bytes 2097168 | tf_op jit(solution)/shard_map/all_gather | solution.py:12
  769.5 29.6 %all-gather.65.cloned.1.call-done = bf16[2048,256]{1,0:T(8,128)(2,1)} async-done(((bf16[512,256]{1,0:T(8,128)(2,1)}), bf16[2048,256]{1,0:T(8,128)(2,1)}) %all-gather.65.cloned.1.call-update) | async-done | bytes 1048592 | tf_op jit(solution)/shard_map/all_gather | solution.py:15
  802.4 25.6 %all-gather.71.cloned.1.call-done = bf16[2048,256]{1,0:T(8,128)(2,1)} async-done(((bf16[512,256]{1,0:T(8,128)(2,1)}), bf16[2048,256]{1,0:T(8,128)(2,1)}) %all-gather.71.cloned.1.call-update) | async-done | bytes 1048592 | tf_op jit(solution)/shard_map/all_gather | solution.py:15
  828.0 29.2 %all-gather.69.cloned.1.call-done = bf16[512,2048]{1,0:T(8,128)(2,1)} async-done(((bf16[512,256]{1,0:T(8,128)(2,1)}), bf16[512,2048]{1,0:T(8,128)(2,1)}) %all-gather.69.cloned.1.call-update) | async-done | bytes 2097168 | tf_op jit(solution)/shard_map/all_gather | solution.py:12
  861.2 26.2 %all-gather.75.cloned.1.call-done = bf16[2048,256]{1,0:T(8,128)(2,1)} async-done(((bf16[512,256]{1,0:T(8,128)(2,1)}), bf16[2048,256]{1,0:T(8,128)(2,1)}) %all-gather.75.cloned.1.call-update) | async-done | bytes 1048592 | tf_op jit(solution)/shard_map/all_gather | solution.py:15
  887.4 29.2 %all-gather.73.cloned.1.call-done = bf16[512,2048]{1,0:T(8,128)(2,1)} async-done(((bf16[512,256]{1,0:T(8,128)(2,1)}), bf16[512,2048]{1,0:T(8,128)(2,1)}) %all-gather.73.cloned.1.call-update) | async-done | bytes 2097168 | tf_op jit(solution)/shard_map/all_gather | solution.py:12
  920.0 27.1 %all-gather.67.cloned.1.call-done = bf16[512,2048]{1,0:T(8,128)(2,1)} async-done(((bf16[512,256]{1,0:T(8,128)(2,1)}), bf16[512,2048]{1,0:T(8,128)(2,1)}) %all-gather.67.cloned.1.call-update) | async-done | bytes 2097168 | tf_op jit(solution)/shard_map/all_gather | solution.py:12
  947.1 29.6 %all-gather.77.cloned.1.call-done = bf16[2048,256]{1,0:T(8,128)(2,1)} async-done(((bf16[512,256]{1,0:T(8,128)(2,1)}), bf16[2048,256]{1,0:T(8,128)(2,1)}) %all-gather.77.cloned.1.call-update) | async-done | bytes 1048592 | tf_op jit(solution)/shard_map/all_gather | solution.py:15
  976.7 4.0 fusion.14
  980.7 40.4 %all-reduce = (f32[]{:T(128)}, f32[]{:T(128)}, f32[]{:T(128)}) all-reduce(f32[]{:T(128)} %get-tuple-element.4, f32[]{:T(128)} %get-tuple-element.12, f32[]{:T(128)} %get-tuple-element.3), channel_id=1, replica_groups=mesh['gx'=4,'gy'=8] {'gx','gy'}, use_global_device_ids=true, to_apply=%region_9.10 | all-reduce | flops 3 | bytes 24 | tf_op jit(solution)/shard_map/psum | solution.py:48
  (88 shorter events, 54.3 us)
Async XLA Ops:
  7.2 137.7 %reduce-scatter.3.cloned.1.call-start = ((), (), s32[]{:S(2)}) async-start(), calls=%async_computation.2 | async-start | bytes 18874368 | tf_op jit(solution)/shard_map/reduce_scatter | solution.py:35
  26.0 118.9 %copy-start = (f32[512,256]{1,0:T(8,128)S(1)}, f32[512,256]{1,0:T(8,128)}, u32[]{:S(2)}) copy-start(f32[512,256]{1,0:T(8,128)} %param.7) | copy-start | bytes 1572868
  26.0 169.0 %reduce-scatter.5.cloned.1.call-start = ((), (), s32[]{:S(2)}) async-start(), calls=%async_computation.3 | async-start | bytes 2621440 | tf_op jit(solution)/shard_map/reduce_scatter | solution.py:36
  144.8 75.8 %all-gather.29.cloned.1.call-start = ((), (), s32[]{:S(2)}) async-start(), calls=%async_computation.5 | async-start | bytes 1310720 | tf_op jit(solution)/shard_map/all_gather | solution.py:15
  146.3 104.1 %all-gather.27.cloned.1.call-start = ((), (), s32[]{:S(2)}) async-start(), calls=%async_computation.4 | async-start | bytes 2359296 | tf_op jit(solution)/shard_map/all_gather | solution.py:12
  146.4 46.5 %copy-start.3 = (f32[2048]{0:T(1024)S(1)}, f32[2048]{0:T(1024)}, u32[]{:S(2)}) copy-start(f32[2048]{0:T(1024)} %param.6) | copy-start | bytes 24580
  194.2 59.5 %copy-start.2 = (f32[2048]{0:T(1024)}, f32[2048]{0:T(1024)S(1)}, u32[]{:S(2)}) copy-start(f32[2048]{0:T(1024)S(1)} %get-tuple-element.11) | copy-start | bytes 24580
  196.9 83.4 %all-gather.33.cloned.1.call-start = ((), (), s32[]{:S(2)}) async-start(), calls=%async_computation.7 | async-start | bytes 2359296 | tf_op jit(solution)/shard_map/all_gather | solution.py:12
  197.5 112.8 %all-gather.31.cloned.1.call-start = ((), (), s32[]{:S(2)}) async-start(), calls=%async_computation.6 | async-start | bytes 1310720 | tf_op jit(solution)/shard_map/all_gather | solution.py:15
  253.7 101.8 %all-gather.37.cloned.1.call-start = ((), (), s32[]{:S(2)}) async-start(), calls=%async_computation.9 | async-start | bytes 2359296 | tf_op jit(solution)/shard_map/all_gather | solution.py:12
  254.7 128.3 %all-gather.39.cloned.1.call-start = ((), (), s32[]{:S(2)}) async-start(), calls=%async_computation.10 | async-start | bytes 1310720 | tf_op jit(solution)/shard_map/all_gather | solution.py:15
  355.5 58.4 %all-gather.41.cloned.1.call-start = ((), (), s32[]{:S(2)}) async-start(), calls=%async_computation.11 | async-start | bytes 1310720 | tf_op jit(solution)/shard_map/all_gather | solution.py:15
  386.3 57.0 %all-gather.35.cloned.1.call-start = ((), (), s32[]{:S(2)}) async-start(), calls=%async_computation.8 | async-start | bytes 2359296 | tf_op jit(solution)/shard_map/all_gather | solution.py:12
  386.9 86.0 %all-gather.47.cloned.1.call-start = ((), (), s32[]{:S(2)}) async-start(), calls=%async_computation.14 | async-start | bytes 1310720 | tf_op jit(solution)/shard_map/all_gather | solution.py:15
  387.7 114.5 %all-gather.45.cloned.1.call-start = ((), (), s32[]{:S(2)}) async-start(), calls=%async_computation.13 | async-start | bytes 2359296 | tf_op jit(solution)/shard_map/all_gather | solution.py:12
  388.2 144.1 %all-gather.51.cloned.1.call-start = ((), (), s32[]{:S(2)}) async-start(), calls=%async_computation.16 | async-start | bytes 1310720 | tf_op jit(solution)/shard_map/all_gather | solution.py:15
  446.7 114.9 %all-gather.49.cloned.1.call-start = ((), (), s32[]{:S(2)}) async-start(), calls=%async_computation.15 | async-start | bytes 2359296 | tf_op jit(solution)/shard_map/all_gather | solution.py:12
  505.5 86.5 %all-gather.43.cloned.1.call-start = ((), (), s32[]{:S(2)}) async-start(), calls=%async_computation.12 | async-start | bytes 2359296 | tf_op jit(solution)/shard_map/all_gather | solution.py:12
  506.1 115.4 %all-gather.53.cloned.1.call-start = ((), (), s32[]{:S(2)}) async-start(), calls=%async_computation.17 | async-start | bytes 1310720 | tf_op jit(solution)/shard_map/all_gather | solution.py:15
  564.9 85.4 %all-gather.59.cloned.1.call-start = ((), (), s32[]{:S(2)}) async-start(), calls=%async_computation.20 | async-start | bytes 1310720 | tf_op jit(solution)/shard_map/all_gather | solution.py:15
  565.5 114.0 %all-gather.57.cloned.1.call-start = ((), (), s32[]{:S(2)}) async-start(), calls=%async_computation.19 | async-start | bytes 2359296 | tf_op jit(solution)/shard_map/all_gather | solution.py:12
  566.0 143.6 %all-gather.63.cloned.1.call-start = ((), (), s32[]{:S(2)}) async-start(), calls=%async_computation.22 | async-start | bytes 1310720 | tf_op jit(solution)/shard_map/all_gather | solution.py:15
  624.7 114.1 %all-gather.61.cloned.1.call-start = ((), (), s32[]{:S(2)}) async-start(), calls=%async_computation.21 | async-start | bytes 2359296 | tf_op jit(solution)/shard_map/all_gather | solution.py:12
  682.8 86.7 %all-gather.55.cloned.1.call-start = ((), (), s32[]{:S(2)}) async-start(), calls=%async_computation.18 | async-start | bytes 2359296 | tf_op jit(solution)/shard_map/all_gather | solution.py:12
  683.5 115.5 %all-gather.65.cloned.1.call-start = ((), (), s32[]{:S(2)}) async-start(), calls=%async_computation.23 | async-start | bytes 1310720 | tf_op jit(solution)/shard_map/all_gather | solution.py:15
  742.2 85.8 %all-gather.71.cloned.1.call-start = ((), (), s32[]{:S(2)}) async-start(), calls=%async_computation.26 | async-start | bytes 1310720 | tf_op jit(solution)/shard_map/all_gather | solution.py:15
  742.9 114.3 %all-gather.69.cloned.1.call-start = ((), (), s32[]{:S(2)}) async-start(), calls=%async_computation.25 | async-start | bytes 2359296 | tf_op jit(solution)/shard_map/all_gather | solution.py:12
  743.5 143.9 %all-gather.75.cloned.1.call-start = ((), (), s32[]{:S(2)}) async-start(), calls=%async_computation.28 | async-start | bytes 1310720 | tf_op jit(solution)/shard_map/all_gather | solution.py:15
  802.3 114.3 %all-gather.73.cloned.1.call-start = ((), (), s32[]{:S(2)}) async-start(), calls=%async_computation.27 | async-start | bytes 2359296 | tf_op jit(solution)/shard_map/all_gather | solution.py:12
  860.5 86.5 %all-gather.67.cloned.1.call-start = ((), (), s32[]{:S(2)}) async-start(), calls=%async_computation.24 | async-start | bytes 2359296 | tf_op jit(solution)/shard_map/all_gather | solution.py:12
  861.1 115.5 %copy-start.1 = (f32[512,256]{1,0:T(8,128)S(1)}, f32[512,256]{1,0:T(8,128)}, u32[]{:S(2)}) copy-start(f32[512,256]{1,0:T(8,128)} %reduce-scatter.5.cloned.1.call-done) | copy-start | bytes 1572868
  861.2 115.5 %all-gather.77.cloned.1.call-start = ((), (), s32[]{:S(2)}) async-start(), calls=%async_computation.29 | async-start | bytes 1310720 | tf_op jit(solution)/shard_map/all_gather | solution.py:15
Sparse Core Ops, SparseCore 0:
  26.1 118.6 reduce-scatter.2
  147.1 44.6 reduce-scatter.4
  193.4 27.1 all-gather.28
  222.9 27.4 all-gather.26
  252.2 28.0 all-gather.32
  282.3 27.9 all-gather.30
  312.2 27.6 all-gather.36
  355.6 27.3 all-gather.38
  386.5 27.3 all-gather.40
  416.2 27.1 all-gather.34
  444.9 27.9 all-gather.46
  474.7 27.4 all-gather.44
  504.3 27.9 all-gather.50
  534.1 27.4 all-gather.48
  563.9 28.0 all-gather.42
  593.4 27.9 all-gather.52
  622.9 27.3 all-gather.58
  652.0 27.4 all-gather.56
  681.6 27.9 all-gather.62
  711.4 27.4 all-gather.60
  741.3 28.0 all-gather.54
  771.0 27.9 all-gather.64
  800.6 27.3 all-gather.70
  829.8 27.4 all-gather.68
  859.4 27.9 all-gather.74
  889.1 27.4 all-gather.72
  919.0 28.0 all-gather.66
  948.7 27.9 all-gather.76
where the time goes:
time: 1030 us
  waiting for transfers between devices  815 us (79%)
  blocking collectives  123 us (12%)
  matrix products  61.5 us (6%)
  between operations  20.3 us (2%)
  other arithmetic  10.5 us (1%)
    all_gather x13, waiting for transfers between devices, product(): lax.all_gather(right_half, 'gx', axis=0, tiled=True)  350 us
    all_gather x13, waiting for transfers between devices, product(): panel = lax.all_gather(left_half, 'gy', axis=1, tiled=True)  339 us
    reduce_scatter x1, waiting for transfers between devices, shards(): lax.psum_scatter(partial_gram, 'gy', scatter_dimension=1, tiled=True)  119 us
    psum x2, blocking collectives, shards(): lax.psum((jnp.sum(prod * prod), jnp.sum(cov_tile * identity_tile), jnp.su...  80.7 us
    dot_general x13, matrix products, product(): jnp.dot(panel, lax.all_gather(right_half, 'gx', axis=0, tiled=True), pref...  43.4 us
    psum x1, blocking collectives, shards(): total, count = lax.psum((column_total, local_count), ('gx', 'gy'))  42.2 us
  transfers between devices with their start and end apart: 28, of which 26 were waited for; matrix products, arithmetic and copies ran while one was open for 5% of the time, Pallas kernels for 0%

commit v1 on v0

--- a/solution.py
+++ b/solution.py
@@ -6,15 +6,32 @@
 ITERS = 4
 
 
+def laid_out(parts, dim):
+    parts = jnp.moveaxis(parts, 0, dim)
+    dims = parts.shape
+    return parts.reshape(*dims[:dim], dims[dim] * dims[dim + 1], *dims[dim + 2 :])
+
+
+def grow_blocks(array, axis):
+    count, here = (lax.axis_size(axis), lax.axis_index(axis))
+    blocks, bit = (array[None], 1)
+    while bit < count:
+        other = lax.ppermute(blocks, axis, [(i, i ^ bit) for i in range(count)])
+        low = here & bit == 0
+        blocks = jnp.concatenate([jnp.where(low, blocks, other), jnp.where(low, other, blocks)])
+        bit *= 2
+    return blocks
+
+
+def doubled_up(x, axis, dim):
+    return laid_out(grow_blocks(x, axis), dim)
+
+
 def product(left, right):
     left_half = left.astype(jnp.bfloat16)
     right_half = right.astype(jnp.bfloat16)
     panel = lax.all_gather(left_half, "gy", axis=1, tiled=True)
-    return jnp.dot(
-        panel,
-        lax.all_gather(right_half, "gx", axis=0, tiled=True),
-        preferred_element_type=jnp.float32,
-    )
+    return jnp.dot(panel, doubled_up(right_half, "gx", 0), preferred_element_type=jnp.float32)
 
 
 def shards(features, counts, ref_mean, ref_root):

time: 1030 us -> 776 us (0.75)
  waiting for transfers between devices: 815 us -> 539 us
  starting transfers between devices: 1.3 us -> 23 us
    ppermute x0 -> x26, waiting for transfers between devices: none -> 392 us  [grow_blocks(): other = lax.ppermute(blocks, axis, [(i, i ^ bit) for i in range(count)])]
    all_gather x13 -> x0, waiting for transfers between devices: 350 us -> none  [product(): lax.all_gather(right_half, 'gx', axis=0, tiled=True)]
    all_gather x13, waiting for transfers between devices: 339 us -> 27.6 us  [product(): panel = lax.all_gather(left_half, 'gy', axis=1, tiled=True)]
    ppermute x0 -> x26, starting transfers between devices: none -> 22.2 us  [grow_blocks(): other = lax.ppermute(blocks, axis, [(i, i ^ bit) for i in range(count)])]
  transfers between devices with their start and end apart: 28 -> 41, of which waited for: 26 -> 27; matrix products, arithmetic and copies ran while one was open for 5% -> 5% of each run, Pallas kernels for 0% -> 0%
where the time goes in v1:
time: 776 us; the launch traced here: 775 us
  waiting for transfers between devices  539 us (69%)
  blocking collectives  119 us (15%)
  matrix products  55.6 us (7%)
  starting transfers between devices  23 us (3%)
  between operations  20.3 us (3%)
  other arithmetic  17.1 us (2%)
    ppermute x26, waiting for transfers between devices, grow_blocks(): other = lax.ppermute(blocks, axis, [(i, i ^ bit) for i in range(count)])  392 us
    reduce_scatter x1, waiting for transfers between devices, shards(): lax.psum_scatter(partial_gram, 'gy', scatter_dimension=1, tiled=True)  119 us
    psum x2, blocking collectives, shards(): lax.psum((jnp.sum(prod * prod), jnp.sum(cov_tile * identity_tile), jnp.su...  76.2 us
    psum x1, blocking collectives, shards(): total, count = lax.psum((column_total, local_count), ('gx', 'gy'))  42.7 us
    dot_general x13, matrix products, product(): jnp.dot(panel, doubled_up(right_half, 'gx', 0), preferred_element_type=jn...  37.4 us
    all_gather x13, waiting for transfers between devices, product(): panel = lax.all_gather(left_half, 'gy', axis=1, tiled=True)  27.6 us
    ppermute x26, starting transfers between devices, grow_blocks(): other = lax.ppermute(blocks, axis, [(i, i ^ bit) for i in range(count)])  22.2 us
    dot_general x1, matrix products, shards(): lax.dot_general(masked, features, (((0,), (0,)), ((), ())), preferred_ele...  18.1 us
  transfers between devices with their start and end apart: 41, of which 27 were waited for; matrix products, arithmetic and copies ran while one was open for 5% of the time, Pallas kernels for 0%

profile of v1, /device:TPU:0, one launch (start us, length us, event | category | flops | bytes accessed | tf_op | source)
XLA Modules:
  0.0 774.8 jit_solution(16098159044122355847)
XLA Ops:
  7.9 18.1 %fusion = f32[2048,2048]{1,0:T(8,128)} fusion(bf16[1280,2048]{1,0:T(8,128)(2,1)} %param.4, pred[1280]{0:T(1024)(128)(4,1)S(1)} %iota_compare_fusion), kind=kOutput, calls=%fused_computation.1 | convolution fusion | flops 10740039680 | bytes 22021376 | tf_op jit(solution)/shard_map/dot_general | solution.py:46
  26.1 118.8 %reduce-scatter.3.cloned.1.call-done = f32[2048,256]{1,0:T(8,128)} async-done(((f32[2048,2048]{1,0:T(8,128)}), f32[2048,256]{1,0:T(8,128)}) %reduce-scatter.3.cloned.1.call-update) | async-done | bytes 2097168 | tf_op jit(solution)/shard_map/reduce_scatter | solution.py:52
  148.6 42.7 %all-reduce.1 = (f32[2048]{0:T(1024)S(1)}, f32[]{:T(128)}) all-reduce(f32[2048]{0:T(1024)S(1)} %convert_reduce_fusion, f32[]{:T(128)S(6)} %convert_element_type.87), channel_id=1, replica_groups=mesh['gx'=4,'gy'=8] {'gx','gy'}, use_global_device_ids=true, to_apply=%region_1.2 | all-reduce | flops 2049 | bytes 16392 | tf_op jit(solution)/shard_map/psum | solution.py:51
  199.1 7.0 collective-permute-done
  209.2 23.3 %collective-permute-done.1 = bf16[2,512,256]{2,1,0:T(8,128)(2,1)S(1)} collective-permute-done((bf16[2,512,256]{2,1,0:T(8,128)(2,1)S(1)}, bf16[2,512,256]{2,1,0:T(8,128)(2,1)S(1)}, u32[]{:S(2)}, u32[]{:S(2)}) %collective-permute-start.1) | collective-permute-done | bytes 524320 | tf_op jit(solution)/shard_map/ppermute | solution.py:19
  236.1 7.1 collective-permute-done.2
  243.6 24.6 %collective-permute-done.3 = bf16[2,512,256]{2,1,0:T(8,128)(2,1)S(1)} collective-permute-done((bf16[2,512,256]{2,1,0:T(8,128)(2,1)S(1)}, bf16[2,512,256]{2,1,0:T(8,128)(2,1)S(1)}, u32[]{:S(2)}, u32[]{:S(2)}) %collective-permute-start.3) | collective-permute-done | bytes 524320 | tf_op jit(solution)/shard_map/ppermute | solution.py:19
  271.4 37.3 %psum.44 = f32[]{:T(128)} all-reduce(f32[]{:T(128)} %get-tuple-element.67), channel_id=1, replica_groups=mesh['gx'=4,'gy'=8] {'gx','gy'}, use_global_device_ids=true, to_apply=%region_6.7 | all-reduce | flops 1 | bytes 8 | tf_op jit(solution)/shard_map/psum | solution.py:65
  312.6 5.7 collective-permute-done.4
  320.3 22.8 %collective-permute-done.5 = bf16[2,512,256]{2,1,0:T(8,128)(2,1)S(1)} collective-permute-done((bf16[2,512,256]{2,1,0:T(8,128)(2,1)S(1)}, bf16[2,512,256]{2,1,0:T(8,128)(2,1)S(1)}, u32[]{:S(2)}, u32[]{:S(2)}) %collective-permute-start.5) | collective-permute-done | bytes 524320 | tf_op jit(solution)/shard_map/ppermute | solution.py:19
  347.4 7.3 collective-permute-done.8
  355.4 23.9 %collective-permute-done.9 = bf16[2,512,256]{2,1,0:T(8,128)(2,1)S(1)} collective-permute-done((bf16[2,512,256]{2,1,0:T(8,128)(2,1)S(1)}, bf16[2,512,256]{2,1,0:T(8,128)(2,1)S(1)}, u32[]{:S(2)}, u32[]{:S(2)}) %collective-permute-start.9) | collective-permute-done | bytes 524320 | tf_op jit(solution)/shard_map/ppermute | solution.py:19
  382.7 8.2 %collective-permute-done.6 = bf16[1,512,256]{2,1,0:T(8,128)(2,1)S(1)} collective-permute-done((bf16[1,512,256]{2,1,0:T(8,128)(2,1)S(1)}, bf16[1,512,256]{2,1,0:T(8,128)(2,1)S(1)}, u32[]{:S(2)}, u32[]{:S(2)}) %collective-permute-start.6) | collective-permute-done | bytes 262176 | tf_op jit(solution)/shard_map/ppermute | solution.py:19
  391.4 24.7 %collective-permute-done.7 = bf16[2,512,256]{2,1,0:T(8,128)(2,1)S(1)} collective-permute-done((bf16[2,512,256]{2,1,0:T(8,128)(2,1)S(1)}, bf16[2,512,256]{2,1,0:T(8,128)(2,1)S(1)}, u32[]{:S(2)}, u32[]{:S(2)}) %collective-permute-start.7) | collective-permute-done | bytes 524320 | tf_op jit(solution)/shard_map/ppermute | solution.py:19
  418.8 8.1 %collective-permute-done.10 = bf16[1,512,256]{2,1,0:T(8,128)(2,1)S(1)} collective-permute-done((bf16[1,512,256]{2,1,0:T(8,128)(2,1)S(1)}, bf16[1,512,256]{2,1,0:T(8,128)(2,1)S(1)}, u32[]{:S(2)}, u32[]{:S(2)}) %collective-permute-start.10) | collective-permute-done | bytes 262176 | tf_op jit(solution)/shard_map/ppermute | solution.py:19
  427.6 24.4 %collective-permute-done.11 = bf16[2,512,256]{2,1,0:T(8,128)(2,1)S(1)} collective-permute-done((bf16[2,512,256]{2,1,0:T(8,128)(2,1)S(1)}, bf16[2,512,256]{2,1,0:T(8,128)(2,1)S(1)}, u32[]{:S(2)}, u32[]{:S(2)}) %collective-permute-start.11) | collective-permute-done | bytes 524320 | tf_op jit(solution)/shard_map/ppermute | solution.py:19
  456.1 8.2 %collective-permute-done.14 = bf16[1,512,256]{2,1,0:T(8,128)(2,1)S(1)} collective-permute-done((bf16[1,512,256]{2,1,0:T(8,128)(2,1)S(1)}, bf16[1,512,256]{2,1,0:T(8,128)(2,1)S(1)}, u32[]{:S(2)}, u32[]{:S(2)}) %collective-permute-start.14) | collective-permute-done | bytes 262176 | tf_op jit(solution)/shard_map/ppermute | solution.py:19
  465.2 24.4 %collective-permute-done.15 = bf16[2,512,256]{2,1,0:T(8,128)(2,1)S(1)} collective-permute-done((bf16[2,512,256]{2,1,0:T(8,128)(2,1)S(1)}, bf16[2,512,256]{2,1,0:T(8,128)(2,1)S(1)}, u32[]{:S(2)}, u32[]{:S(2)}) %collective-permute-start.15) | collective-permute-done | bytes 524320 | tf_op jit(solution)/shard_map/ppermute | solution.py:19
  493.0 8.2 %collective-permute-done.12 = bf16[1,512,256]{2,1,0:T(8,128)(2,1)S(1)} collective-permute-done((bf16[1,512,256]{2,1,0:T(8,128)(2,1)S(1)}, bf16[1,512,256]{2,1,0:T(8,128)(2,1)S(1)}, u32[]{:S(2)}, u32[]{:S(2)}) %collective-permute-start.12) | collective-permute-done | bytes 262176 | tf_op jit(solution)/shard_map/ppermute | solution.py:19
  502.1 24.4 %collective-permute-done.13 = bf16[2,512,256]{2,1,0:T(8,128)(2,1)S(1)} collective-permute-done((bf16[2,512,256]{2,1,0:T(8,128)(2,1)S(1)}, bf16[2,512,256]{2,1,0:T(8,128)(2,1)S(1)}, u32[]{:S(2)}, u32[]{:S(2)}) %collective-permute-start.13) | collective-permute-done | bytes 524320 | tf_op jit(solution)/shard_map/ppermute | solution.py:19
  529.9 8.4 %collective-permute-done.16 = bf16[1,512,256]{2,1,0:T(8,128)(2,1)S(1)} collective-permute-done((bf16[1,512,256]{2,1,0:T(8,128)(2,1)}, bf16[1,512,256]{2,1,0:T(8,128)(2,1)S(1)}, u32[]{:S(2)}, u32[]{:S(2)}) %collective-permute-start.16) | collective-permute-done | bytes 262176 | tf_op jit(solution)/shard_map/ppermute | solution.py:19
  540.2 24.3 %collective-permute-done.17 = bf16[2,512,256]{2,1,0:T(8,128)(2,1)S(1)} collective-permute-done((bf16[2,512,256]{2,1,0:T(8,128)(2,1)S(1)}, bf16[2,512,256]{2,1,0:T(8,128)(2,1)S(1)}, u32[]{:S(2)}, u32[]{:S(2)}) %collective-permute-start.17) | collective-permute-done | bytes 524320 | tf_op jit(solution)/shard_map/ppermute | solution.py:19
  568.0 8.4 %collective-permute-done.18 = bf16[1,512,256]{2,1,0:T(8,128)(2,1)S(1)} collective-permute-done((bf16[1,512,256]{2,1,0:T(8,128)(2,1)}, bf16[1,512,256]{2,1,0:T(8,128)(2,1)S(1)}, u32[]{:S(2)}, u32[]{:S(2)}) %collective-permute-start.18) | collective-permute-done | bytes 262176 | tf_op jit(solution)/shard_map/ppermute | solution.py:19
  580.0 22.7 %collective-permute-done.19 = bf16[2,512,256]{2,1,0:T(8,128)(2,1)S(1)} collective-permute-done((bf16[2,512,256]{2,1,0:T(8,128)(2,1)S(1)}, bf16[2,512,256]{2,1,0:T(8,128)(2,1)S(1)}, u32[]{:S(2)}, u32[]{:S(2)}) %collective-permute-start.19) | collective-permute-done | bytes 524320 | tf_op jit(solution)/shard_map/ppermute | solution.py:19
  607.9 10.3 %collective-permute-done.22 = bf16[1,512,256]{2,1,0:T(8,128)(2,1)S(1)} collective-permute-done((bf16[1,512,256]{2,1,0:T(8,128)(2,1)S(1)}, bf16[1,512,256]{2,1,0:T(8,128)(2,1)S(1)}, u32[]{:S(2)}, u32[]{:S(2)}) %collective-permute-start.22) | collective-permute-done | bytes 262176 | tf_op jit(solution)/shard_map/ppermute | solution.py:19
  618.5 25.3 %collective-permute-done.21 = bf16[2,512,256]{2,1,0:T(8,128)(2,1)S(1)} collective-permute-done((bf16[2,512,256]{2,1,0:T(8,128)(2,1)S(1)}, bf16[2,512,256]{2,1,0:T(8,128)(2,1)S(1)}, u32[]{:S(2)}, u32[]{:S(2)}) %collective-permute-start.21) | collective-permute-done | bytes 524320 | tf_op jit(solution)/shard_map/ppermute | solution.py:19
  643.8 10.2 %collective-permute-done.23 = bf16[2,512,256]{2,1,0:T(8,128)(2,1)S(1)} collective-permute-done((bf16[2,512,256]{2,1,0:T(8,128)(2,1)S(1)}, bf16[2,512,256]{2,1,0:T(8,128)(2,1)S(1)}, u32[]{:S(2)}, u32[]{:S(2)}) %collective-permute-start.23) | collective-permute-done | bytes 524320 | tf_op jit(solution)/shard_map/ppermute | solution.py:19
  658.0 27.3 %all-gather.38.cloned.1.call-done = bf16[512,2048]{1,0:T(8,128)(2,1)} async-done(((bf16[512,256]{1,0:T(8,128)(2,1)}), bf16[512,2048]{1,0:T(8,128)(2,1)}) %all-gather.38.cloned.1.call-update) | async-done | bytes 2097168 | tf_op jit(solution)/shard_map/all_gather | solution.py:33
  689.2 7.0 collective-permute-done.24
  698.8 22.9 %collective-permute-done.25 = bf16[2,512,256]{2,1,0:T(8,128)(2,1)S(1)} collective-permute-done((bf16[2,512,256]{2,1,0:T(8,128)(2,1)S(1)}, bf16[2,512,256]{2,1,0:T(8,128)(2,1)S(1)}, u32[]{:S(2)}, u32[]{:S(2)}) %collective-permute-start.25) | collective-permute-done | bytes 524320 | tf_op jit(solution)/shard_map/ppermute | solution.py:19
  721.9 3.8 fusion.16
  725.7 38.9 %all-reduce = (f32[]{:T(128)}, f32[]{:T(128)}, f32[]{:T(128)}) all-reduce(f32[]{:T(128)} %get-tuple-element.4, f32[]{:T(128)} %get-tuple-element.38, f32[]{:T(128)} %get-tuple-element.3), channel_id=1, replica_groups=mesh['gx'=4,'gy'=8] {'gx','gy'}, use_global_device_ids=true, to_apply=%region_9.10 | all-reduce | flops 3 | bytes 24 | tf_op jit(solution)/shard_map/psum | solution.py:65
  (167 shorter events, 75.4 us)
Async XLA Ops:
  7.2 137.7 %reduce-scatter.3.cloned.1.call-start = ((), (), s32[]{:S(2)}) async-start(), calls=%async_computation.2 | async-start | bytes 18874368 | tf_op jit(solution)/shard_map/reduce_scatter | solution.py:52
  26.0 168.0 %reduce-scatter.5.cloned.1.call-start = ((), (), s32[]{:S(2)}) async-start(), calls=%async_computation.3 | async-start | bytes 2621440 | tf_op jit(solution)/shard_map/reduce_scatter | solution.py:53
  144.9 87.8 %all-gather.14.cloned.1.call-start = ((), (), s32[]{:S(2)}) async-start(), calls=%async_computation.4 | async-start | bytes 2359296 | tf_op jit(solution)/shard_map/all_gather | solution.py:33
  196.0 72.4 %all-gather.16.cloned.1.call-start = ((), (), s32[]{:S(2)}) async-start(), calls=%async_computation.5 | async-start | bytes 2359296 | tf_op jit(solution)/shard_map/all_gather | solution.py:33
  197.4 145.8 %all-gather.20.cloned.1.call-start = ((), (), s32[]{:S(2)}) async-start(), calls=%async_computation.7 | async-start | bytes 2359296 | tf_op jit(solution)/shard_map/all_gather | solution.py:33
  197.5 8.6 %collective-permute-start = (bf16[1,512,256]{2,1,0:T(8,128)(2,1)}, bf16[1,512,256]{2,1,0:T(8,128)(2,1)S(1)}, u32[]{:S(2)}, u32[]{:S(2)}) collective-permute-start(bf16[1,512,256]{2,1,0:T(8,128)(2,1)} %bitcast.81), channel_id=1, source_target_pairs={{0,8},{8,0},{16,24},{24,16},{1,9},{9,1},{17,25},{25,17},{2,10},{10... | collective-permute-start | bytes 786440 | tf_op jit(solution)/shard_map/ppermute | solution.py:19
  207.2 25.3 %collective-permute-start.1 = (bf16[2,512,256]{2,1,0:T(8,128)(2,1)S(1)}, bf16[2,512,256]{2,1,0:T(8,128)(2,1)S(1)}, u32[]{:S(2)}, u32[]{:S(2)}) collective-permute-start(bf16[2,512,256]{2,1,0:T(8,128)(2,1)S(1)} %pad_maximum_fusion.13), channel_id=1, source_target_pairs={{0,16},{8,24},{16,0},{24,8},{1,17},{9,25},{17,1},{25,9},{2,18},{10... | collective-permute-start | bytes 1572872 | tf_op jit(solution)/shard_map/ppermute | solution.py:19
  236.0 143.4 %all-gather.24.cloned.1.call-start = ((), (), s32[]{:S(2)}) async-start(), calls=%async_computation.9 | async-start | bytes 2359296 | tf_op jit(solution)/shard_map/all_gather | solution.py:33
  243.2 25.0 %collective-permute-start.3 = (bf16[2,512,256]{2,1,0:T(8,128)(2,1)S(1)}, bf16[2,512,256]{2,1,0:T(8,128)(2,1)S(1)}, u32[]{:S(2)}, u32[]{:S(2)}) collective-permute-start(bf16[2,512,256]{2,1,0:T(8,128)(2,1)S(1)} %pad_maximum_fusion.14), channel_id=1, source_target_pairs={{0,16},{8,24},{16,0},{24,8},{1,17},{9,25},{17,1},{25,9},{2,18},{10... | collective-permute-start | bytes 1572872 | tf_op jit(solution)/shard_map/ppermute | solution.py:19
  309.7 8.6 %collective-permute-start.4 = (bf16[1,512,256]{2,1,0:T(8,128)(2,1)S(1)}, bf16[1,512,256]{2,1,0:T(8,128)(2,1)S(1)}, u32[]{:S(2)}, u32[]{:S(2)}) collective-permute-start(bf16[1,512,256]{2,1,0:T(8,128)(2,1)S(1)} %fusion.46), channel_id=1, source_target_pairs={{0,8},{8,0},{16,24},{24,16},{1,9},{9,1},{17,25},{25,17},{2,10},{10... | collective-permute-start | bytes 786440 | tf_op jit(solution)/shard_map/ppermute | solution.py:19
  318.4 24.7 %collective-permute-start.5 = (bf16[2,512,256]{2,1,0:T(8,128)(2,1)S(1)}, bf16[2,512,256]{2,1,0:T(8,128)(2,1)S(1)}, u32[]{:S(2)}, u32[]{:S(2)}) collective-permute-start(bf16[2,512,256]{2,1,0:T(8,128)(2,1)S(1)} %pad_maximum_fusion.15), channel_id=1, source_target_pairs={{0,16},{8,24},{16,0},{24,8},{1,17},{9,25},{17,1},{25,9},{2,18},{10... | collective-permute-start | bytes 1572872 | tf_op jit(solution)/shard_map/ppermute | solution.py:19
  346.3 70.1 %all-gather.18.cloned.1.call-start = ((), (), s32[]{:S(2)}) async-start(), calls=%async_computation.6 | async-start | bytes 2359296 | tf_op jit(solution)/shard_map/all_gather | solution.py:33
  347.1 105.1 %all-gather.26.cloned.1.call-start = ((), (), s32[]{:S(2)}) async-start(), calls=%async_computation.10 | async-start | bytes 2359296 | tf_op jit(solution)/shard_map/all_gather | solution.py:33
  355.0 24.3 %collective-permute-start.9 = (bf16[2,512,256]{2,1,0:T(8,128)(2,1)S(1)}, bf16[2,512,256]{2,1,0:T(8,128)(2,1)S(1)}, u32[]{:S(2)}, u32[]{:S(2)}) collective-permute-start(bf16[2,512,256]{2,1,0:T(8,128)(2,1)S(1)} %pad_maximum_fusion.17), channel_id=1, source_target_pairs={{0,16},{8,24},{16,0},{24,8},{1,17},{9,25},{17,1},{25,9},{2,18},{10... | collective-permute-start | bytes 1572872 | tf_op jit(solution)/shard_map/ppermute | solution.py:19
  382.6 107.2 %all-gather.30.cloned.1.call-start = ((), (), s32[]{:S(2)}) async-start(), calls=%async_computation.12 | async-start | bytes 2359296 | tf_op jit(solution)/shard_map/all_gather | solution.py:33
  391.0 25.2 %collective-permute-start.7 = (bf16[2,512,256]{2,1,0:T(8,128)(2,1)S(1)}, bf16[2,512,256]{2,1,0:T(8,128)(2,1)S(1)}, u32[]{:S(2)}, u32[]{:S(2)}) collective-permute-start(bf16[2,512,256]{2,1,0:T(8,128)(2,1)S(1)} %pad_maximum_fusion.16), channel_id=1, source_target_pairs={{0,16},{8,24},{16,0},{24,8},{1,17},{9,25},{17,1},{25,9},{2,18},{10... | collective-permute-start | bytes 1572872 | tf_op jit(solution)/shard_map/ppermute | solution.py:19
  427.0 25.1 %collective-permute-start.11 = (bf16[2,512,256]{2,1,0:T(8,128)(2,1)S(1)}, bf16[2,512,256]{2,1,0:T(8,128)(2,1)S(1)}, u32[]{:S(2)}, u32[]{:S(2)}) collective-permute-start(bf16[2,512,256]{2,1,0:T(8,128)(2,1)S(1)} %pad_maximum_fusion.18), channel_id=1, source_target_pairs={{0,16},{8,24},{16,0},{24,8},{1,17},{9,25},{17,1},{25,9},{2,18},{10... | collective-permute-start | bytes 1572872 | tf_op jit(solution)/shard_map/ppermute | solution.py:19
  455.4 71.3 %all-gather.22.cloned.1.call-start = ((), (), s32[]{:S(2)}) async-start(), calls=%async_computation.8 | async-start | bytes 2359296 | tf_op jit(solution)/shard_map/all_gather | solution.py:33
  456.0 108.8 %all-gather.32.cloned.1.call-start = ((), (), s32[]{:S(2)}) async-start(), calls=%async_computation.13 | async-start | bytes 2359296 | tf_op jit(solution)/shard_map/all_gather | solution.py:33
  464.4 25.2 %collective-permute-start.15 = (bf16[2,512,256]{2,1,0:T(8,128)(2,1)S(1)}, bf16[2,512,256]{2,1,0:T(8,128)(2,1)S(1)}, u32[]{:S(2)}, u32[]{:S(2)}) collective-permute-start(bf16[2,512,256]{2,1,0:T(8,128)(2,1)S(1)} %pad_maximum_fusion.20), channel_id=1, source_target_pairs={{0,16},{8,24},{16,0},{24,8},{1,17},{9,25},{17,1},{25,9},{2,18},{10... | collective-permute-start | bytes 1572872 | tf_op jit(solution)/shard_map/ppermute | solution.py:19
  492.9 110.0 %all-gather.28.cloned.1.call-start = ((), (), s32[]{:S(2)}) async-start(), calls=%async_computation.11 | async-start | bytes 2359296 | tf_op jit(solution)/shard_map/all_gather | solution.py:33
  501.3 25.2 %collective-permute-start.13 = (bf16[2,512,256]{2,1,0:T(8,128)(2,1)S(1)}, bf16[2,512,256]{2,1,0:T(8,128)(2,1)S(1)}, u32[]{:S(2)}, u32[]{:S(2)}) collective-permute-start(bf16[2,512,256]{2,1,0:T(8,128)(2,1)S(1)} %pad_maximum_fusion.19), channel_id=1, source_target_pairs={{0,16},{8,24},{16,0},{24,8},{1,17},{9,25},{17,1},{25,9},{2,18},{10... | collective-permute-start | bytes 1572872 | tf_op jit(solution)/shard_map/ppermute | solution.py:19
  529.8 124.5 %all-gather.36.cloned.1.call-start = ((), (), s32[]{:S(2)}) async-start(), calls=%async_computation.15 | async-start | bytes 2359296 | tf_op jit(solution)/shard_map/all_gather | solution.py:33
  539.4 25.2 %collective-permute-start.17 = (bf16[2,512,256]{2,1,0:T(8,128)(2,1)S(1)}, bf16[2,512,256]{2,1,0:T(8,128)(2,1)S(1)}, u32[]{:S(2)}, u32[]{:S(2)}) collective-permute-start(bf16[2,512,256]{2,1,0:T(8,128)(2,1)S(1)} %pad_maximum_fusion.21), channel_id=1, source_target_pairs={{0,16},{8,24},{16,0},{24,8},{1,17},{9,25},{17,1},{25,9},{2,18},{10... | collective-permute-start | bytes 1572872 | tf_op jit(solution)/shard_map/ppermute | solution.py:19
  567.9 117.4 %all-gather.38.cloned.1.call-start = ((), (), s32[]{:S(2)}) async-start(), calls=%async_computation.16 | async-start | bytes 2359296 | tf_op jit(solution)/shard_map/all_gather | solution.py:33
  577.5 25.2 %collective-permute-start.19 = (bf16[2,512,256]{2,1,0:T(8,128)(2,1)S(1)}, bf16[2,512,256]{2,1,0:T(8,128)(2,1)S(1)}, u32[]{:S(2)}, u32[]{:S(2)}) collective-permute-start(bf16[2,512,256]{2,1,0:T(8,128)(2,1)S(1)} %pad_maximum_fusion.22), channel_id=1, source_target_pairs={{0,16},{8,24},{16,0},{24,8},{1,17},{9,25},{17,1},{25,9},{2,18},{10... | collective-permute-start | bytes 1572872 | tf_op jit(solution)/shard_map/ppermute | solution.py:19
  578.3 27.1 %collective-permute-start.20 = (bf16[1,512,256]{2,1,0:T(8,128)(2,1)S(1)}, bf16[1,512,256]{2,1,0:T(8,128)(2,1)S(1)}, u32[]{:S(2)}, u32[]{:S(2)}) collective-permute-start(bf16[1,512,256]{2,1,0:T(8,128)(2,1)S(1)} %bitcast.95), channel_id=1, source_target_pairs={{0,8},{8,0},{16,24},{24,16},{1,9},{9,1},{17,25},{25,17},{2,10},{10... | collective-permute-start | bytes 786440 | tf_op jit(solution)/shard_map/ppermute | solution.py:19
  605.3 12.9 %collective-permute-start.22 = (bf16[1,512,256]{2,1,0:T(8,128)(2,1)S(1)}, bf16[1,512,256]{2,1,0:T(8,128)(2,1)S(1)}, u32[]{:S(2)}, u32[]{:S(2)}) collective-permute-start(bf16[1,512,256]{2,1,0:T(8,128)(2,1)S(1)} %bitcast.97), channel_id=1, source_target_pairs={{0,8},{8,0},{16,24},{24,16},{1,9},{9,1},{17,25},{25,17},{2,10},{10... | collective-permute-start | bytes 786440 | tf_op jit(solution)/shard_map/ppermute | solution.py:19
  605.5 38.2 %collective-permute-start.21 = (bf16[2,512,256]{2,1,0:T(8,128)(2,1)S(1)}, bf16[2,512,256]{2,1,0:T(8,128)(2,1)S(1)}, u32[]{:S(2)}, u32[]{:S(2)}) collective-permute-start(bf16[2,512,256]{2,1,0:T(8,128)(2,1)S(1)} %pad_maximum_fusion.23), channel_id=1, source_target_pairs={{0,16},{8,24},{16,0},{24,8},{1,17},{9,25},{17,1},{25,9},{2,18},{10... | collective-permute-start | bytes 1572872 | tf_op jit(solution)/shard_map/ppermute | solution.py:19
  618.4 35.7 %collective-permute-start.23 = (bf16[2,512,256]{2,1,0:T(8,128)(2,1)S(1)}, bf16[2,512,256]{2,1,0:T(8,128)(2,1)S(1)}, u32[]{:S(2)}, u32[]{:S(2)}) collective-permute-start(bf16[2,512,256]{2,1,0:T(8,128)(2,1)S(1)} %pad_maximum_fusion.24), channel_id=1, source_target_pairs={{0,16},{8,24},{16,0},{24,8},{1,17},{9,25},{17,1},{25,9},{2,18},{10... | collective-permute-start | bytes 1572872 | tf_op jit(solution)/shard_map/ppermute | solution.py:19
  657.3 64.6 %all-gather.34.cloned.1.call-start = ((), (), s32[]{:S(2)}) async-start(), calls=%async_computation.14 | async-start | bytes 2359296 | tf_op jit(solution)/shard_map/all_gather | solution.py:33
  696.3 25.4 %collective-permute-start.25 = (bf16[2,512,256]{2,1,0:T(8,128)(2,1)S(1)}, bf16[2,512,256]{2,1,0:T(8,128)(2,1)S(1)}, u32[]{:S(2)}, u32[]{:S(2)}) collective-permute-start(bf16[2,512,256]{2,1,0:T(8,128)(2,1)S(1)} %pad_maximum_fusion.25), channel_id=1, source_target_pairs={{0,16},{8,24},{16,0},{24,8},{1,17},{9,25},{17,1},{25,9},{2,18},{10... | collective-permute-start | bytes 1572872 | tf_op jit(solution)/shard_map/ppermute | solution.py:19
  (19 other events, 276.2 us)
Sparse Core Ops, SparseCore 0:
  26.2 118.6 reduce-scatter.2
  147.2 44.6 reduce-scatter.4
  196.1 28.6 all-gather.13
  226.6 28.0 all-gather.15
  257.0 28.2 all-gather.19
  346.4 27.0 all-gather.23
  376.0 28.0 all-gather.17
  406.0 28.0 all-gather.25
  455.5 27.9 all-gather.29
  485.8 28.0 all-gather.21
  515.9 28.0 all-gather.31
  546.3 28.0 all-gather.27
  576.3 28.0 all-gather.35
  657.4 27.8 all-gather.37
  687.6 28.0 all-gather.33
